TPU v7x, 32 devices: a whole 2x2x4 slice. The times are simulated.
32 devices in a mesh: grp: 2 (over x), tm: 16 (over z, y, core).
Axes of the slice: x: 2, y: 2, z: 4, core: 2. Of those that a mesh axis runs over, the one named last changes fastest.
Arguments:
- samples: bfloat16 [16, 2097152], P('grp', 'tm'), parts along dimension 0, may hold values from -128 to 127, as said below
- filter_taps: bfloat16 [16, 8192], replicated, may hold values from -4 to 4
Outputs:
- channelized: bfloat16 [16, 2, 4096, 256], P('grp', None, 'tm'), parts along dimension 0
There are 2 independent parts, one for each index of `grp`. A program takes and returns all parts, laid end to end along the dimension named above; an argument that names none is the same for every part. Nothing has to cross between parts.
Inputs may be any that keep to these rules, and one draw needn't show every extreme that they name: `samples`: every sample is a whole number, as from an 8-bit converter.
All inputs are finite; a program needn't handle non-finite values.
Results may differ from a plain program's by a relative error of at most 0.007.
Values may be sent and summed in bfloat16 or wider, within the bound.
A program may use at most 128 MiB of HBM per device.

v0:
```python
import jax
import jax.numpy as jnp
from jax import lax
from jax.sharding import PartitionSpec as P

ROW_LEN = 128
target_level = 0.378
epsilon = 1e-06


def shifted(value, axis, by):
    size = lax.axis_size(axis)
    pairs = [(i, i + by) for i in range(size) if 0 <= i + by < size]
    return lax.ppermute(value, axis, pairs)


def tables(row_len, col_len):
    fft_len = row_len * col_len
    rows_a = jnp.arange(row_len, dtype=jnp.int32)
    cols_b = jnp.arange(col_len, dtype=jnp.int32)
    half_c = jnp.arange(col_len // 2, dtype=jnp.int32)
    angle_a = (
        2.0 * jnp.pi / row_len * (rows_a[:, None] * rows_a[None, :] % row_len).astype(jnp.float32)
    )
    angle_t = (
        2.0 * jnp.pi / fft_len * (cols_b[:, None] * rows_a[None, :] % fft_len).astype(jnp.float32)
    )
    angle_b = (
        2.0 * jnp.pi / col_len * (cols_b[:, None] * half_c[None, :] % col_len).astype(jnp.float32)
    )
    return (
        jnp.cos(angle_a).astype(jnp.bfloat16),
        jnp.sin(angle_a).astype(jnp.bfloat16),
        jnp.cos(angle_t),
        jnp.sin(angle_t),
        jnp.cos(angle_b).astype(jnp.bfloat16),
        jnp.sin(angle_b).astype(jnp.bfloat16),
    )


def transform(filtered):
    streams, frames, fft_len = filtered.shape
    col_len = fft_len // ROW_LEN
    cos_a, sin_a, cos_t, sin_t, cos_b, sin_b = tables(ROW_LEN, col_len)
    blocks = filtered.reshape(streams, frames, ROW_LEN, col_len)
    first_re = jnp.einsum("sfab,ad->sfbd", blocks, cos_a, preferred_element_type=jnp.float32)
    first_im = -jnp.einsum("sfab,ad->sfbd", blocks, sin_a, preferred_element_type=jnp.float32)
    twisted_re = (first_re * cos_t + first_im * sin_t).astype(jnp.bfloat16)
    twisted_im = (first_im * cos_t - first_re * sin_t).astype(jnp.bfloat16)
    spec_re = jnp.einsum(
        "sfbd,bc->scdf", twisted_re, cos_b, preferred_element_type=jnp.float32
    ) + jnp.einsum("sfbd,bc->scdf", twisted_im, sin_b, preferred_element_type=jnp.float32)
    spec_im = jnp.einsum(
        "sfbd,bc->scdf", twisted_im, cos_b, preferred_element_type=jnp.float32
    ) - jnp.einsum("sfbd,bc->scdf", twisted_re, sin_b, preferred_element_type=jnp.float32)
    return (spec_re.reshape(streams, -1, frames), spec_im.reshape(streams, -1, frames))


def on_device(samples, filter_taps):
    streams = samples.shape[0]
    tap_count, fft_len = filter_taps.shape
    frames = samples.shape[1] // fft_len
    signal = samples.reshape(streams, frames, fft_len)
    history = shifted(signal[:, frames - (tap_count - 1) :, :], "tm", 1)
    extended = jnp.concatenate([history, signal], axis=1)
    weights = filter_taps.astype(jnp.float32)
    filtered = jnp.zeros((streams, frames, fft_len), jnp.float32)
    for tap_index in range(tap_count):
        offset = tap_count - 1 - tap_index
        filtered = filtered + weights[tap_index] * extended[:, offset : offset + frames].astype(
            jnp.float32
        )
    filtered = filtered.astype(jnp.bfloat16)
    spec_re, spec_im = transform(filtered)
    real_part = spec_re.astype(jnp.bfloat16)
    imag_part = spec_im.astype(jnp.bfloat16)
    real_wide = real_part.astype(jnp.float32)
    imag_wide = imag_part.astype(jnp.float32)
    local_power = jnp.sum(real_wide * real_wide + imag_wide * imag_wide, axis=(1, 2))
    total_power = lax.psum(local_power, "tm")
    count = frames * lax.axis_size("tm") * spec_re.shape[1]
    gain = target_level / jnp.sqrt(total_power / count + epsilon)
    scaled = jnp.stack(
        [
            jnp.clip(real_wide * gain[:, None, None], -1.0, 1.0),
            jnp.clip(imag_wide * gain[:, None, None], -1.0, 1.0),
        ],
        axis=1,
    ).astype(jnp.bfloat16)
    result = lax.all_to_all(scaled, "tm", split_axis=2, concat_axis=3, tiled=True)
    return result


def solution(mesh):
    return jax.shard_map(
        on_device,
        mesh=mesh,
        in_specs=(P("grp", "tm"), P()),
        out_specs=P("grp", None, "tm", None),
        check_vma=False,
    )
```

profile of v0, /device:TPU:1, one launch (start us, length us, event | category | flops | bytes accessed | tf_op | source)
XLA Modules:
  0.0 244.5 jit_solution(3988610349749079119)
XLA Ops:
  0.0 0.0 copy-start.2
  0.0 0.0 copy-start.1
  0.0 1.8 slice.130
  1.8 4.5 %collective-permute-start = (bf16[8,15,8192]{2,0,1:T(8,128)(2,1)S(1)}, bf16[8,15,8192]{2,0,1:T(8,128)(2,1)S(1)}, u32[]{:S(2)}, u32[]{:S(2)}) collective-permute-start(bf16[8,15,8192]{2,0,1:T(8,128)(2,1)S(1)} %slice.130), channel_id=1, source_target_pairs={{0,1},{1,2},{2,3},{3,4},{4,5},{5,6},{6,7},{7,8},{8,9},{9,10},{10,1... | collective-permute-start | bytes 5898248 | tf_op jit(solution)/shard_map/ppermute | solution.py:14
  6.4 0.1 fusion.43
  6.5 0.0 copy-done.2
  6.5 0.5 fusion.80
  7.0 20.9 %collective-permute-done = bf16[8,15,8192]{2,0,1:T(8,128)(2,1)S(1)} collective-permute-done((bf16[8,15,8192]{2,0,1:T(8,128)(2,1)S(1)}, bf16[8,15,8192]{2,0,1:T(8,128)(2,1)S(1)}, u32[]{:S(2)}, u32[]{:S(2)}) %collective-permute-start) | collective-permute-done | bytes 1966112 | tf_op jit(solution)/shard_map/ppermute | solution.py:14
  27.9 0.0 copy-done.1
  27.9 8.7 %add_convert_fusion.1 = bf16[8,16,8192]{2,0,1:T(8,128)(2,1)S(1)} fusion(bf16[8,16,8192]{2,0,1:T(8,128)(2,1)S(1)} %bitcast.84, bf16[8,15,8192]{2,0,1:T(8,128)(2,1)S(1)} %collective-permute-done, f32[8192]{0:T(1024)S(1)} %bitcast.100, f32[8192]{0:T(1024)S(1)} %bitcast.99, f32[8192]{0:T(1024)S(1)} %bitcast.98, f32[8192]{0:T(1024)S(1)} %bitcast.97, ...), kind=kLoop, calls=%fused_computation.30 | loop fusion | flops 66060288 | bytes 6684672 | tf_op jit(solution)/shard_map/convert_element_type | solution.py:73
  36.6 1.2 copy.27
  37.8 5.5 %reshape.106 = bf16[8,16,128,64]{3,2,1,0:T(8,128)(2,1)} reshape(bf16[8,16,8192]{2,1,0:T(8,128)(2,1)S(1)} %copy.27) | data formatting | bytes 4194304 | tf_op jit(solution)/shard_map/reshape | solution.py:45
  43.3 0.0 copy-start
  43.3 3.7 %fusion.33 = f32[8,16,64,128]{3,2,1,0:T(8,128)S(1)} fusion(bf16[8,16,128,64]{3,2,1,0:T(8,128)(2,1)} %reshape.106), kind=kOutput, calls=%fused_computation.81 | convolution fusion | flops 268681216 | bytes 6291456 | tf_op jit(solution)/shard_map/sfab,ad->sfbd/dot_general | solution.py:47
  47.0 0.0 copy-done
  47.0 1.7 add_convert_fusion
  48.8 0.5 fusion.54
  49.3 0.5 fusion.52
  49.8 0.5 add_convert_fusion.2
  50.3 1.6 convert_bitcast_fusion
  51.9 0.8 fusion.1
  52.7 30.6 %psum.7 = f32[8]{0:T(128)S(1)} all-reduce(f32[8]{0:T(128)S(1)} %get-tuple-element.25), channel_id=1, replica_groups=mesh['grp'=2,'tm'=16] {'tm'}, use_global_device_ids=true, to_apply=%region_1.2 | all-reduce | flops 8 | bytes 64 | tf_op jit(solution)/shard_map/psum | solution.py:80
  83.4 1.8 reshape.107
  85.1 1.6 convert_bitcast_fusion.1
  86.7 2.7 %reshape.108 = f32[8,1,4096,16]{2,3,0,1:T(8,128)} reshape(f32[8,32,128,16]{2,1,3,0:T(8,128)} %convert_bitcast_fusion.1) | data formatting | bytes 4194304 | tf_op jit(solution)/shard_map/convert_element_type | solution.py:78
  89.5 2.0 fusion.19
  91.5 0.2 pad_maximum_fusion.1
  91.7 27.8 %copy.32 = bf16[8,2,4096,16]{3,1,0,2:T(2,128)(2,1)} copy(bf16[8,2,4096,16]{2,3,1,0:T(8,128)(2,1)S(1)} %pad_maximum_fusion.1) | data formatting | bytes 4194304 | tf_op jit(solution)/shard_map/stack | solution.py:83
  119.5 19.7 %reshape.113 = bf16[16,2,32768]{2,1,0:T(2,128)(2,1)S(1)} reshape(bf16[4096,8,2,16]{3,2,1,0:T(2,128)(2,1)} %bitcast.80) | data formatting | bytes 4194304
  139.3 51.1 %all_to_all.18 = bf16[16,2,32768]{2,1,0:T(2,128)(2,1)} all-to-all(bf16[16,2,32768]{2,1,0:T(2,128)(2,1)S(1)} %reshape.113), channel_id=1, replica_groups=mesh['grp'=2,'tm'=16] {'tm'}, dimensions={0} | all-to-all | bytes 4194304 | tf_op jit(solution)/shard_map/all_to_all | solution.py:90
  190.4 16.5 %reshape.114 = bf16[4096,8,2,16]{3,2,1,0:T(2,128)(2,1)} reshape(bf16[16,2,32768]{2,1,0:T(2,128)(2,1)} %all_to_all.18) | data formatting | bytes 4194304
  206.8 35.3 %copy.43 = bf16[8,2,16,256,16]{3,4,2,1,0:T(8,128)(2,1)S(1)} copy(bf16[8,2,16,256,16]{4,1,0,3,2:T(2,128)(2,1)} %bitcast.81) | data formatting | bytes 4194304 | tf_op jit(solution)/shard_map/all_to_all | solution.py:90
  242.1 2.4 copy.35
  (1 shorter events, 0.0 us)
Async XLA Ops:
  0.0 6.5 %copy-start.2 = (bf16[16,8192]{1,0:T(8,128)(2,1)S(1)}, bf16[16,8192]{1,0:T(8,128)(2,1)}, u32[]{:S(2)}) copy-start(bf16[16,8192]{1,0:T(8,128)(2,1)} %param.3) | copy-start | bytes 786436
  0.0 27.9 %copy-start.1 = (bf16[8,131072]{1,0:T(8,128)(2,1)S(1)}, bf16[8,131072]{1,0:T(8,128)(2,1)}, u32[]{:S(2)}) copy-start(bf16[8,131072]{1,0:T(8,128)(2,1)} %param.2) | copy-start | bytes 6291460
  1.8 26.1 %collective-permute-start = (bf16[8,15,8192]{2,0,1:T(8,128)(2,1)S(1)}, bf16[8,15,8192]{2,0,1:T(8,128)(2,1)S(1)}, u32[]{:S(2)}, u32[]{:S(2)}) collective-permute-start(bf16[8,15,8192]{2,0,1:T(8,128)(2,1)S(1)} %slice.130), channel_id=1, source_target_pairs={{0,1},{1,2},{2,3},{3,4},{4,5},{5,6},{6,7},{7,8},{8,9},{9,10},{10,1... | collective-permute-start | bytes 5898248 | tf_op jit(solution)/shard_map/ppermute | solution.py:14
  43.3 3.7 %copy-start = (bf16[8,16,128,64]{3,2,1,0:T(8,128)(2,1)S(1)}, bf16[8,16,128,64]{3,2,1,0:T(8,128)(2,1)}, u32[]{:S(2)}) copy-start(bf16[8,16,128,64]{3,2,1,0:T(8,128)(2,1)} %reshape.106) | copy-start | bytes 6291460
where the time goes:
time: 246 us; the launch traced here: 244 us
  local copies, waits for them, and re-layouts  115 us (47%)
  blocking collectives  81.7 us (33%)
  waiting for transfers between devices  20.9 us (8%)
  other arithmetic  14.3 us (6%)
  matrix products  7.76 us (3%)
  starting transfers between devices  4.53 us (2%)
    all_to_all x1, blocking collectives, on_device(): lax.all_to_all(scaled, 'tm', split_axis=2, concat_axis=3, tiled=True)  51.1 us
    all_to_all x2, local copies, waits for them, and re-layouts, on_device(): lax.all_to_all(scaled, 'tm', split_axis=2, concat_axis=3, tiled=True)  37.7 us
    unnamed x8, local copies, waits for them, and re-layouts  36.2 us
    psum x1, blocking collectives, on_device(): total_power = lax.psum(local_power, 'tm')  30.6 us
    another operation x1, local copies, waits for them, and re-layouts, on_device(): jnp.stack([jnp.clip(real_wide * gain[:, None, None], -1.0, 1.0), jnp.clip...  27.8 us
    ppermute x1, waiting for transfers between devices, shifted(): return lax.ppermute(value, axis, pairs)  20.9 us
    convert_element_type x1, other arithmetic, on_device(): filtered = filtered.astype(jnp.bfloat16)  8.7 us
    reshape x1, local copies, waits for them, and re-layouts, transform(): blocks = filtered.reshape(streams, frames, ROW_LEN, col_len)  5.54 us
  transfers between devices with their start and end apart: 1, of which 1 were waited for; matrix products, arithmetic and copies ran while one was open for 0% of the time, Pallas kernels for 0%

commit v1 on v0

--- a/solution.py
+++ b/solution.py
@@ -77,7 +77,11 @@
     real_wide = real_part.astype(jnp.float32)
     imag_wide = imag_part.astype(jnp.float32)
     local_power = jnp.sum(real_wide * real_wide + imag_wide * imag_wide, axis=(1, 2))
-    total_power = lax.psum(local_power, "tm")
+
+    def choose_rings(base_x):
+        return lax.all_gather(base_x, "tm").sum(axis=0)
+
+    total_power = choose_rings(local_power)
     count = frames * lax.axis_size("tm") * spec_re.shape[1]
     gain = target_level / jnp.sqrt(total_power / count + epsilon)
     scaled = jnp.stack(

time: 246 us -> 255 us (1.037)
  other arithmetic: 14.3 us -> 20.9 us
    psum x1 -> x0, blocking collectives: 30.6 us -> none  [on_device(): total_power = lax.psum(local_power, 'tm')]
    unnamed x0 -> x1, blocking collectives: none -> 30.6 us
    convert_element_type x1, other arithmetic: 8.7 us -> 15.3 us  [on_device(): filtered = filtered.astype(jnp.bfloat16)]
    unnamed x8 -> x13, local copies, waits for them, and re-layouts: 36.2 us -> 37.1 us
  transfers between devices with their start and end apart: 1 -> 1, of which waited for: 1 -> 1; matrix products, arithmetic and copies ran while one was open for 0% -> 1% of each run, Pallas kernels for 0% -> 0%
where the time goes in v1:
time: 255 us; the launch traced here: 253 us
  local copies, waits for them, and re-layouts  117 us (46%)
  blocking collectives  81.7 us (32%)
  other arithmetic  20.9 us (8%)
  waiting for transfers between devices  19.9 us (8%)
  matrix products  7.77 us (3%)
  starting transfers between devices  4.52 us (2%)
    all_to_all x1, blocking collectives, on_device(): lax.all_to_all(scaled, 'tm', split_axis=2, concat_axis=3, tiled=True)  51.1 us
    all_to_all x2, local copies, waits for them, and re-layouts, on_device(): lax.all_to_all(scaled, 'tm', split_axis=2, concat_axis=3, tiled=True)  37.7 us
    unnamed x13, local copies, waits for them, and re-layouts  37.1 us
    unnamed x1, blocking collectives  30.6 us
    another operation x1, local copies, waits for them, and re-layouts, on_device(): jnp.stack([jnp.clip(real_wide * gain[:, None, None], -1.0, 1.0), jnp.clip...  27.8 us
    ppermute x1, waiting for transfers between devices, shifted(): return lax.ppermute(value, axis, pairs)  19.9 us
    convert_element_type x1, other arithmetic, on_device(): filtered = filtered.astype(jnp.bfloat16)  15.3 us
    reshape x1, local copies, waits for them, and re-layouts, transform(): blocks = filtered.reshape(streams, frames, ROW_LEN, col_len)  5.53 us
  transfers between devices with their start and end apart: 1, of which 1 were waited for; matrix products, arithmetic and copies ran while one was open for 1% of the time, Pallas kernels for 0%

profile of v1, /device:TPU:1, one launch (start us, length us, event | category | flops | bytes accessed | tf_op | source)
XLA Modules:
  0.0 253.0 jit_solution(13952734660045768836)
XLA Ops:
  0.0 0.0 copy-start.3
  0.0 0.0 copy-start.2
  0.0 0.0 copy-start.1
  0.0 3.1 %slice.130 = bf16[8,15,8192]{2,0,1:T(8,128)(2,1)} slice(bf16[8,16,8192]{2,0,1:T(8,128)(2,1)} %bitcast.84), slice={[0:8], [1:16], [0:8192]} | slice | bytes 3932160 | tf_op jit(solution)/shard_map/slice | solution.py:64
  3.2 4.5 %collective-permute-start = (bf16[8,15,8192]{2,0,1:T(8,128)(2,1)}, bf16[8,15,8192]{2,0,1:T(8,128)(2,1)}, u32[]{:S(2)}, u32[]{:S(2)}) collective-permute-start(bf16[8,15,8192]{2,0,1:T(8,128)(2,1)} %slice.130), channel_id=1, source_target_pairs={{0,1},{1,2},{2,3},{3,4},{4,5},{5,6},{6,7},{7,8},{8,9},{9,10},{10,1... | collective-permute-start | bytes 5898248 | tf_op jit(solution)/shard_map/ppermute | solution.py:14
  7.7 0.0 copy-done.3
  7.7 0.7 dynamic-slice
  9.1 0.1 fusion.43
  9.2 0.0 copy-done.2
  9.2 0.5 fusion.80
  9.7 19.9 %collective-permute-done = bf16[8,15,8192]{2,0,1:T(8,128)(2,1)} collective-permute-done((bf16[8,15,8192]{2,0,1:T(8,128)(2,1)}, bf16[8,15,8192]{2,0,1:T(8,128)(2,1)}, u32[]{:S(2)}, u32[]{:S(2)}) %collective-permute-start) | collective-permute-done | bytes 1966112 | tf_op jit(solution)/shard_map/ppermute | solution.py:14
  29.5 0.0 copy-done.1
  29.6 15.3 %add_convert_fusion.1 = bf16[8,16,8192]{2,0,1:T(8,128)(2,1)S(1)} fusion(bf16[8,16,8192]{2,0,1:T(8,128)(2,1)S(1)} %bitcast.85, bf16[8,15,8192]{2,0,1:T(8,128)(2,1)} %collective-permute-done, f32[8192]{0:T(1024)S(1)} %bitcast.101, f32[8192]{0:T(1024)S(1)} %bitcast.100, f32[8192]{0:T(1024)S(1)} %bitcast.99, f32[8192]{0:T(1024)S(1)} %bitcast.98, ...), kind=kLoop, calls=%fused_computation.30 | loop fusion | flops 66060288 | bytes 6684672 | tf_op jit(solution)/shard_map/convert_element_type | solution.py:73
  44.8 1.2 copy.27
  46.0 5.5 %reshape.111 = bf16[8,16,128,64]{3,2,1,0:T(8,128)(2,1)} reshape(bf16[8,16,8192]{2,1,0:T(8,128)(2,1)S(1)} %copy.27) | data formatting | bytes 4194304 | tf_op jit(solution)/shard_map/reshape | solution.py:45
  51.5 0.0 copy-start
  51.5 3.7 %fusion.33 = f32[8,16,64,128]{3,2,1,0:T(8,128)S(1)} fusion(bf16[8,16,128,64]{3,2,1,0:T(8,128)(2,1)} %reshape.111), kind=kOutput, calls=%fused_computation.81 | convolution fusion | flops 268681216 | bytes 6291456 | tf_op jit(solution)/shard_map/sfab,ad->sfbd/dot_general | solution.py:47
  55.2 0.0 copy-done
  55.2 1.7 add_convert_fusion
  56.9 0.5 fusion.54
  57.4 0.5 fusion.52
  58.0 0.5 add_convert_fusion.2
  58.5 1.6 convert_bitcast_fusion
  60.1 0.8 fusion.1
  60.9 0.2 dynamic-update-slice
  61.1 30.6 %all-reduce = f32[128]{0:T(128)S(1)} all-reduce(f32[128]{0:T(128)S(1)} %dynamic-update-slice), channel_id=2, replica_groups=mesh['grp'=2,'tm'=16] {'tm'}, use_global_device_ids=true, to_apply=%add | all-reduce | flops 128 | bytes 1024
  91.7 0.1 reshape.114
  91.8 1.8 reshape.112
  93.6 1.6 convert_bitcast_fusion.1
  95.2 2.8 %reshape.113 = f32[8,1,4096,16]{2,3,0,1:T(8,128)} reshape(f32[8,32,128,16]{2,1,3,0:T(8,128)} %convert_bitcast_fusion.1) | data formatting | bytes 4194304 | tf_op jit(solution)/shard_map/convert_element_type | solution.py:78
  98.0 2.0 fusion.19
  100.0 0.2 pad_maximum_fusion.1
  100.2 27.8 %copy.32 = bf16[8,2,4096,16]{3,1,0,2:T(2,128)(2,1)} copy(bf16[8,2,4096,16]{2,3,1,0:T(8,128)(2,1)S(1)} %pad_maximum_fusion.1) | data formatting | bytes 4194304 | tf_op jit(solution)/shard_map/stack | solution.py:87
  128.0 19.7 %reshape.124 = bf16[16,2,32768]{2,1,0:T(2,128)(2,1)S(1)} reshape(bf16[4096,8,2,16]{3,2,1,0:T(2,128)(2,1)} %bitcast.81) | data formatting | bytes 4194304
  147.8 51.1 %all_to_all.18 = bf16[16,2,32768]{2,1,0:T(2,128)(2,1)} all-to-all(bf16[16,2,32768]{2,1,0:T(2,128)(2,1)S(1)} %reshape.124), channel_id=1, replica_groups=mesh['grp'=2,'tm'=16] {'tm'}, dimensions={0} | all-to-all | bytes 4194304 | tf_op jit(solution)/shard_map/all_to_all | solution.py:94
  198.9 16.5 %reshape.125 = bf16[4096,8,2,16]{3,2,1,0:T(2,128)(2,1)} reshape(bf16[16,2,32768]{2,1,0:T(2,128)(2,1)} %all_to_all.18) | data formatting | bytes 4194304
  215.3 35.3 %copy.43 = bf16[8,2,16,256,16]{3,4,2,1,0:T(8,128)(2,1)S(1)} copy(bf16[8,2,16,256,16]{4,1,0,3,2:T(2,128)(2,1)} %bitcast.82) | data formatting | bytes 4194304 | tf_op jit(solution)/shard_map/all_to_all | solution.py:94
  250.6 2.4 copy.35
  (3 shorter events, 0.0 us)
Async XLA Ops:
  0.0 7.7 %copy-start.3 = (u32[32]{0:T(128)S(1)}, u32[32]{0:T(128)}, u32[]{:S(2)}) copy-start(u32[32]{0:T(128)} %constant.64) | copy-start | bytes 388
  0.0 9.2 %copy-start.2 = (bf16[16,8192]{1,0:T(8,128)(2,1)S(1)}, bf16[16,8192]{1,0:T(8,128)(2,1)}, u32[]{:S(2)}) copy-start(bf16[16,8192]{1,0:T(8,128)(2,1)} %param.3) | copy-start | bytes 786436
  0.0 29.5 %copy-start.1 = (bf16[8,131072]{1,0:T(8,128)(2,1)S(1)}, bf16[8,131072]{1,0:T(8,128)(2,1)}, u32[]{:S(2)}) copy-start(bf16[8,131072]{1,0:T(8,128)(2,1)} %param.2) | copy-start | bytes 6291460
  3.2 26.4 %collective-permute-start = (bf16[8,15,8192]{2,0,1:T(8,128)(2,1)}, bf16[8,15,8192]{2,0,1:T(8,128)(2,1)}, u32[]{:S(2)}, u32[]{:S(2)}) collective-permute-start(bf16[8,15,8192]{2,0,1:T(8,128)(2,1)} %slice.130), channel_id=1, source_target_pairs={{0,1},{1,2},{2,3},{3,4},{4,5},{5,6},{6,7},{7,8},{8,9},{9,10},{10,1... | collective-permute-start | bytes 5898248 | tf_op jit(solution)/shard_map/ppermute | solution.py:14
  51.5 3.7 %copy-start = (bf16[8,16,128,64]{3,2,1,0:T(8,128)(2,1)S(1)}, bf16[8,16,128,64]{3,2,1,0:T(8,128)(2,1)}, u32[]{:S(2)}) copy-start(bf16[8,16,128,64]{3,2,1,0:T(8,128)(2,1)} %reshape.111) | copy-start | bytes 6291460
